TPU v7x, 32 devices: a whole 2x2x4 slice. The times are simulated.
32 devices in a mesh: row: 8 (over z, core), col: 4 (over y, x).
Axes of the slice: x: 2, y: 2, z: 4, core: 2. Of those that a mesh axis runs over, the one named last changes fastest.
Arguments:
- df_blocks: bfloat16 [576, 576, 1024], P('row', 'col'), may hold values from -1 to 1
- amplitudes: bfloat16 [48, 576, 576], P(None, 'col'), may hold values from -0.009765625 to 0.009765625
Outputs:
- ladder_ab: float32 [576, 4, 48], P('row')
- ladder_ba: float32 [576, 4, 48], P('row')
All inputs are finite; a program needn't handle non-finite values.
Results may differ from a plain program's by a relative error of at most 0.0029.
Values may be sent and summed in bfloat16 or wider, within the bound.
A program may use at most 192 MiB of HBM per device.

v0:
```python
import functools

import jax
import jax.numpy as jnp
from jax import lax
from jax.experimental import pallas as pl
from jax.experimental.pallas import tpu as pltpu
from jax.sharding import PartitionSpec as P

WIN = 4
LANES = 128
NT = (((1,), (1,)), ((), ()))


def shifted_2(value, axis, steps):
    count = lax.axis_size(axis)
    pairs = [(source, (source + steps) % count) for source in range(count)]
    return lax.ppermute(value, axis, pairs)


def ladder_kernel(rows, whole, rest, rows_ref, window_ref, amps_ref, out_ref, tile):
    group = amps_ref.shape[0]

    @pl.when(pl.program_id(0) == 0)
    def _():
        out_ref[...] = jnp.zeros_like(out_ref)

    resident = rows_ref[...]

    def one(j, carry):
        at = pl.multiple_of(j * whole, LANES)
        tile[:, pl.ds(at, whole)] = lax.dot_general(
            resident, window_ref[pl.ds(at, whole), :], NT, preferred_element_type=jnp.float32
        )
        return carry

    lax.fori_loop(0, WIN, one, 0)
    if rest:
        tile[:, WIN * whole:] = lax.dot_general(
            resident, window_ref[WIN * whole:, :], NT, preferred_element_type=jnp.float32
        )
        owner = lax.broadcasted_iota(jnp.int32, (rows, WIN * rest), 1) // rest
    total = out_ref[...]
    for c in range(group):
        at = slice(c * rows, (c + 1) * rows)
        parts = []
        for j in range(WIN):
            part = tile[at, j * whole:(j + 1) * whole]
            if rest:
                tail = jnp.where(owner == j, tile[at, WIN * whole:], 0.0)
                part = jnp.concatenate([part, tail], axis=1)
            parts.append(part)
        stacked = jnp.concatenate(parts, axis=0).astype(jnp.bfloat16)
        total += lax.dot_general(stacked, amps_ref[c], NT, preferred_element_type=jnp.float32)
    out_ref[...] = total


def ladder(by_c, window, amps, group):
    columns, rows, depth = by_c.shape
    pairs2, width = amps.shape[1:]
    extent = window.shape[0] // WIN
    whole = extent // LANES * LANES
    rest = extent - whole
    flat = by_c.reshape(columns * rows, depth)
    return pl.pallas_call(
        functools.partial(ladder_kernel, rows, whole, rest),
        grid=(columns // group,),
        out_shape=jax.ShapeDtypeStruct((WIN * rows, pairs2), jnp.float32),
        in_specs=[
            pl.BlockSpec((group * rows, depth), lambda i: (i, 0)),
            pl.BlockSpec((WIN * extent, depth), lambda i: (0, 0)),
            pl.BlockSpec((group, pairs2, width), lambda i: (i, 0, 0)),
        ],
        out_specs=pl.BlockSpec((WIN * rows, pairs2), lambda i: (0, 0)),
        scratch_shapes=[pltpu.VMEM((group * rows, WIN * extent), jnp.float32)],
        compiler_params=pltpu.CompilerParams(
            dimension_semantics=("arbitrary",), vmem_limit_bytes=60 * 1024 * 1024
        ),
        cost_estimate=pl.CostEstimate(
            flops=2 * columns * rows * WIN * extent * (depth + pairs2),
            bytes_accessed=2 * (flat.size + window.size + amps.size),
            transcendentals=0,
        ),
    )(flat, window, amps)


def shards(df_blocks, amplitudes):
    rows, columns, depth = df_blocks.shape
    pairs, _, extent = amplitudes.shape
    row_count = lax.axis_size("row")
    shifted = shifted_2(df_blocks[:WIN], "row", -1)
    window = lax.all_gather(shifted, "col", axis=1, tiled=True)
    if pairs % row_count == 0:
        share = pairs // row_count
        own = lax.dynamic_slice_in_dim(amplitudes, lax.axis_index("row") * share, share, 0)
        own = lax.all_to_all(own, "col", split_axis=2, concat_axis=1, tiled=True)
        own = own.transpose(0, 2, 1)
        flipped = lax.all_gather(own, "row", axis=0, tiled=True).transpose(1, 0, 2)
    else:
        flipped = lax.all_to_all(amplitudes, "col", split_axis=2, concat_axis=1, tiled=True)
        flipped = flipped.transpose(2, 0, 1)
    amps = jnp.concatenate([amplitudes.transpose(1, 0, 2), flipped], axis=1)
    whole = extent // LANES * LANES
    if extent > whole:
        amps = jnp.concatenate([amps[:, :, :whole]] + [amps[:, :, whole:]] * WIN, axis=2)
        window = jnp.concatenate(
            [window[:, :whole].reshape(-1, depth), window[:, whole:].reshape(-1, depth)], axis=0
        )
    else:
        window = window.reshape(-1, depth)
    by_c = df_blocks.transpose(1, 0, 2)
    group = next(g for g in (8, 6, 4, 2, 1) if columns % g == 0 and (g * rows % 16 == 0 or g == 1))
    total = ladder(by_c, window, amps, group)
    total = lax.psum(total, "col").reshape(WIN, rows, 2 * pairs).transpose(1, 0, 2)
    return (total[:, :, :pairs], total[:, :, pairs:])


def solution(mesh):
    in_specs = (P("row", "col", None), P(None, "col", None))
    out_specs = (P("row", None, None), P("row", None, None))
    return jax.shard_map(shards, mesh=mesh, in_specs=in_specs, out_specs=out_specs, check_vma=False)
```

profile of v0, /device:TPU:0, one launch (start us, length us, event | category | flops | bytes accessed | tf_op | source)
XLA Modules:
  0.0 385.5 jit_solution(2481357582157873069)
XLA Ops:
  7.2 0.0 all-gather.3.cloned.1.call-start
  7.2 1.4 slice.20
  8.6 4.6 %collective-permute-start = (bf16[4,144,1024]{2,1,0:T(8,128)(2,1)S(1)}, bf16[4,144,1024]{2,1,0:T(8,128)(2,1)S(1)}, u32[]{:S(2)}, u32[]{:S(2)}) collective-permute-start(bf16[4,144,1024]{2,1,0:T(8,128)(2,1)S(1)} %slice.20), channel_id=1, source_target_pairs={{0,28},{4,0},{8,4},{12,8},{16,12},{20,16},{24,20},{28,24},{1,29},{... | collective-permute-start | bytes 3538952 | tf_op jit(solution)/shard_map/ppermute | solution.py:18
  13.1 13.7 %collective-permute-done = bf16[4,144,1024]{2,1,0:T(8,128)(2,1)S(1)} collective-permute-done((bf16[4,144,1024]{2,1,0:T(8,128)(2,1)S(1)}, bf16[4,144,1024]{2,1,0:T(8,128)(2,1)S(1)}, u32[]{:S(2)}, u32[]{:S(2)}) %collective-permute-start) | collective-permute-done | bytes 1179680 | tf_op jit(solution)/shard_map/ppermute | solution.py:18
  26.9 0.0 copy-start.1
  26.9 1.0 copy-done.1
  27.9 0.0 all-gather.3.cloned.1.call-update
  27.9 0.0 all-gather.5.cloned.1.call-start
  27.9 1.3 constant_dynamic-slice_fusion
  29.3 3.0 copy.19
  32.3 3.5 reshape.20
  35.8 28.1 %all_to_all.18 = bf16[4,2,62208]{2,1,0:T(2,128)(2,1)} all-to-all(bf16[4,2,62208]{2,1,0:T(2,128)(2,1)S(1)} %reshape.20), channel_id=1, replica_groups=mesh['row'=8,'col'=4] {'col'}, dimensions={0} | all-to-all | bytes 1990656 | tf_op jit(solution)/shard_map/all_to_all | solution.py:96
  63.9 4.9 %reshape.21 = bf16[576,6,144]{2,1,0:T(8,128)(2,1)S(1)} reshape(bf16[4,2,62208]{2,1,0:T(2,128)(2,1)} %all_to_all.18) | data formatting | bytes 1990656
  68.8 2.6 copy.25
  71.4 4.2 %all_to_all.16 = bf16[6,576,144]{1,2,0:T(8,128)(2,1)} reshape(bf16[6,4,144,144]{2,1,3,0:T(4,128)(2,1)} %bitcast.31) | data formatting | bytes 1990656 | tf_op jit(solution)/shard_map/all_to_all | solution.py:96
  75.6 0.0 all-gather.5.cloned.1.call-update
  75.7 0.0 all-reduce.2.cloned.1.call-start
  75.7 8.8 %copy.24 = bf16[48,144,576]{2,0,1:T(8,128)(2,1)} copy(bf16[48,144,576]{2,1,0:T(8,128)(2,1)} %param.3) | data formatting | bytes 15925248 | tf_op args[1]
  84.5 30.2 %copy.13 = bf16[144,72,1024]{2,1,0:T(8,128)(2,1)} copy(bf16[144,72,1024]{2,0,1:T(8,128)(2,1)} %bitcast.25) | data formatting | bytes 42467328 | tf_op jit(solution)/shard_map/transpose | solution.py:111
  114.8 0.0 all-gather.3.cloned.1.call-done
  114.8 0.0 slice-start
  114.8 0.0 slice-start.1
  114.8 1.0 slice-done
  115.8 1.3 slice-done.1
  117.1 2.6 pad_maximum_fusion.1.window_ref
  119.8 64.5 %all-gather.5.cloned.1.call-done = bf16[48,144,576]{2,1,0:T(8,128)(2,1)} async-done(((bf16[6,144,576]{2,1,0:T(8,128)(2,1)}), bf16[48,144,576]{2,1,0:T(8,128)(2,1)}) %all-gather.5.cloned.1.call-update) | async-done | bytes 7962640 | tf_op jit(solution)/shard_map/all_gather | solution.py:98
  184.3 8.9 %copy.23 = bf16[48,144,576]{2,0,1:T(8,128)(2,1)} copy(bf16[48,144,576]{2,1,0:T(8,128)(2,1)} %all-gather.5.cloned.1.call-done) | data formatting | bytes 15925248 | tf_op jit(solution)/shard_map/all_gather | solution.py:98
  193.1 0.0 copy-start
  193.1 2.9 pad_maximum_fusion.2
  196.0 1.7 copy-done
  197.7 36.1 %pad_maximum_fusion.amps_ref = bf16[144,96,768]{2,1,0:T(8,128)(2,1)} fusion(bf16[144,96,64]{2,1,0:T(8,128)(2,1)S(1)} %pad_maximum_fusion.2, bf16[144,48,576]{2,1,0:T(8,128)(2,1)S(1)} %bitcast.24, bf16[144,48,576]{2,1,0:T(8,128)(2,1)} %bitcast.22), kind=kLoop, calls=%fused_computation | loop fusion | flops 106168320 | bytes 38928384 | tf_op jit(solution)/shard_map/concatenate | solution.py:105
  233.8 100.6 %shard_map.41 = f32[288,96]{1,0:T(8,128)} custom-call(bf16[10368,1024]{1,0:T(8,128)(2,1)} %bitcast.26, bf16[2304,1024]{1,0:T(8,128)(2,1)} %pad_maximum_fusion.1.window_ref, bf16[144,96,768]{2,1,0:T(8,128)(2,1)} %pad_maximum_fusion.amps_ref), custom_call_target="tpu_custom_call" | custom-call | flops 53508833280 | bytes 47185920 | tf_op jit(solution)/shard_map/pallas_call | solution.py:65
  334.4 1.7 copy.18
  336.1 0.0 all-reduce.2.cloned.1.call-update
  336.1 41.2 %all-reduce.2.cloned.1.call-done = f32[72,4,96]{0,2,1:T(8,128)} async-done(((f32[72,4,96]{0,2,1:T(8,128)}), f32[72,4,96]{0,2,1:T(8,128)}) %all-reduce.2.cloned.1.call-update) | async-done | bytes 110608 | tf_op jit(solution)/shard_map/psum | solution.py:114
  377.3 1.6 fusion
Async XLA Ops:
  7.2 107.6 %all-gather.3.cloned.1.call-start = ((), (), s32[]{:S(2)}) async-start(), calls=%async_computation.1 | async-start | bytes 5898240 | tf_op jit(solution)/shard_map/all_gather | solution.py:92
  8.6 18.3 %collective-permute-start = (bf16[4,144,1024]{2,1,0:T(8,128)(2,1)S(1)}, bf16[4,144,1024]{2,1,0:T(8,128)(2,1)S(1)}, u32[]{:S(2)}, u32[]{:S(2)}) collective-permute-start(bf16[4,144,1024]{2,1,0:T(8,128)(2,1)S(1)} %slice.20), channel_id=1, source_target_pairs={{0,28},{4,0},{8,4},{12,8},{16,12},{20,16},{24,20},{28,24},{1,29},{... | collective-permute-start | bytes 3538952 | tf_op jit(solution)/shard_map/ppermute | solution.py:18
  26.9 1.0 copy-start.1
  27.9 156.4 %all-gather.5.cloned.1.call-start = ((), (), s32[]{:S(2)}) async-start(), calls=%async_computation.2 | async-start | bytes 9953280 | tf_op jit(solution)/shard_map/all_gather | solution.py:98
  75.7 301.7 %all-reduce.2.cloned.1.call-start = ((), (), s32[]{:S(2)}) async-start(), calls=%async_computation.3 | async-start | bytes 393216 | tf_op jit(solution)/shard_map/psum | solution.py:114
  114.8 1.0 slice-start
  114.8 2.4 slice-start.1
  193.1 4.6 %copy-start = (bf16[48,144,576]{2,0,1:T(8,128)(2,1)S(1)}, bf16[48,144,576]{2,0,1:T(8,128)(2,1)}, u32[]{:S(2)}) copy-start(bf16[48,144,576]{2,0,1:T(8,128)(2,1)} %copy.23) | copy-start | bytes 23887876
Sparse Core Ops, SparseCore 0:
  28.0 68.7 all-gather.2
  98.4 85.8 all-gather.4
  336.2 41.0 all-reduce.1
where the time goes:
time: 386 us; the launch traced here: 385 us
  waiting for transfers between devices  119 us (31%)
  Pallas kernels  101 us (26%)
  local copies, waits for them, and re-layouts  77.3 us (20%)
  other arithmetic  41.6 us (11%)
  blocking collectives  28.1 us (7%)
  between operations  13.8 us (4%)
  starting transfers between devices  4.69 us (1%)
    pallas_call x1, Pallas kernels, ladder(): pl.pallas_call(functools.partial(ladder_kernel, rows, whole, rest), grid=...  101 us
    all_gather x1, waiting for transfers between devices, shards(): flipped = lax.all_gather(own, 'row', axis=0, tiled=True).transpose(1, 0, 2)  64.5 us
    psum x1, waiting for transfers between devices, shards(): lax.psum(total, 'col').reshape(WIN, rows, 2 * pairs).transpose(1, 0, 2)  41.2 us
    concatenate x1, other arithmetic, shards(): jnp.concatenate([amps[:, :, :whole]] + [amps[:, :, whole:]] * WIN, axis=2)  36.1 us
    transpose x1, local copies, waits for them, and re-layouts, shards(): by_c = df_blocks.transpose(1, 0, 2)  30.2 us
    all_to_all x1, blocking collectives, shards(): own = lax.all_to_all(own, 'col', split_axis=2, concat_axis=1, tiled=True)  28.1 us
    unnamed x8, local copies, waits for them, and re-layouts  23 us
    ppermute x1, waiting for transfers between devices, shifted_2(): return lax.ppermute(value, axis, pairs)  13.7 us
  transfers between devices with their start and end apart: 4, of which 3 were waited for; matrix products, arithmetic and copies ran while one was open for 15% of the time, Pallas kernels for 0%

commit v1 on v0

--- a/solution.py
+++ b/solution.py
@@ -84,7 +84,340 @@
     )(flat, window, amps)
 
 
+NN = pl.DeviceIdType.MESH
+GROUP = 16
+SHARES = 4
+
+
+def matmul_nt(lhs, rhs):
+    return lax.dot_general(lhs, rhs, NT, preferred_element_type=jnp.float32)
+
+
+def fused_kernel(
+    row_count, col_count, df_ref, amps_ref, flip_ref, flip_tail_ref, out_ref,
+    slabs, window, tiled, direct, direct_tail, flipped, flipped_tail, stage_b, stage_t, parts,
+    own_s, own_r, near_s, near_r, far_s, far_r, share_s, share_r, relay_s, relay_r, pair_s, pair_r,
+    tail_s, tail_r, sum_s, sum_r, local, stage_b_sem, stage_t_sem,
+):
+    rows, columns, depth = df_ref.shape
+    pairs = amps_ref.shape[0]
+    extra = columns - LANES
+    chunks = columns // GROUP
+    span = GROUP * rows
+    share = columns // SHARES
+    octets = flip_tail_ref.shape[0] // col_count
+    r, q = lax.axis_index("row"), lax.axis_index("col")
+    below, above = lax.rem(r + row_count - 1, row_count), lax.rem(r + 1, row_count)
+    slot_r = lax.rem(r, SHARES)
+    odd = lax.rem(r, 2)
+    mate = r + 1 - 2 * odd
+    upper = lax.rem(r // 2, 2)
+    twin = r + 2 - 4 * upper
+    qx, qy = lax.rem(q, 2), q // 2
+    x_q = qy * 2 + (1 - qx)
+    y_q = (1 - qy) * 2 + qx
+    d_q = (1 - qy) * 2 + (1 - qx)
+    peers = (q, x_q, y_q, d_q)
+
+    def remote(src, dst, send, recv, dr, dq):
+        return pltpu.make_async_remote_copy(
+            src_ref=src, dst_ref=dst, send_sem=send, recv_sem=recv, device_id=(dr, dq), device_id_type=NN
+        )
+
+    def own(j):
+        return remote(df_ref.at[j], window.at[0, j], own_s.at[j], own_r.at[j], below, q)
+
+    def near(k, j):
+        return remote(window.at[0, j], window.at[k, j], near_s.at[k - 1, j], near_r.at[k - 1, j], r, peers[k])
+
+    def far(j):
+        k = 1 if j < 2 else 2
+        return remote(window.at[k, j], window.at[3, j], far_s.at[j], far_r.at[j], r, peers[3 - k])
+
+    def share_at(s):
+        return pl.ds(s * share, share)
+
+    def shared(k):
+        src = flip_ref.at[pl.ds(peers[k] * columns + slot_r * share, share)]
+        return remote(src, flipped.at[k, share_at(slot_r)], share_s.at[k - 1], share_r.at[k - 1], r, peers[k])
+
+    def relay(k):
+        ref = flipped.at[k, share_at(slot_r)]
+        return remote(ref, ref, relay_s.at[k - 1], relay_r.at[k - 1], twin, q)
+
+    def pair(k, h):
+        s = slot_r if h == 0 else lax.rem(twin, SHARES)
+        ref = flipped.at[k, share_at(s)]
+        return remote(ref, ref, pair_s.at[k - 1, h], pair_r.at[k - 1, h], mate, q)
+
+    def tails(k):
+        src = flip_tail_ref.at[pl.ds(peers[k] * octets, octets)]
+        return remote(src, flipped_tail.at[k], tail_s.at[k - 1], tail_r.at[k - 1], r, peers[k])
+
+    def sums(k):
+        return remote(out_ref, parts.at[k - 1], sum_s.at[k - 1], sum_r.at[k - 1], r, peers[k])
+
+    def fetch_b(i, slot):
+        at = pl.multiple_of(i * GROUP, GROUP)
+        return pltpu.make_async_copy(df_ref.at[:, pl.ds(at, GROUP), :], stage_b.at[slot], stage_b_sem.at[slot])
+
+    def fetch_t(i, slot):
+        at = pl.multiple_of(i * GROUP, GROUP)
+        return pltpu.make_async_copy(amps_ref.at[:, pl.ds(at, GROUP), :], stage_t.at[slot], stage_t_sem.at[slot])
+
+    fetch_t(0, 0).start()
+    fetch_b(0, 0).start()
+    own_flip = pltpu.make_async_copy(flip_ref.at[pl.ds(q * columns, columns)], flipped.at[0], local.at[0])
+    own_tail = pltpu.make_async_copy(flip_tail_ref.at[pl.ds(q * octets, octets)], flipped_tail.at[0], local.at[1])
+    own_flip.start()
+    own_tail.start()
+
+    barrier = pltpu.get_barrier_semaphore()
+    for dr, dq in ((below, q), (above, q), (twin, q), (r, x_q), (r, y_q), (r, d_q)):
+        pl.semaphore_signal(barrier, inc=1, device_id=(dr, dq), device_id_type=NN)
+    pl.semaphore_wait(barrier, 6)
+
+    for j in range(WIN):
+        own(j).start()
+    shared(1).start()
+    shared(2).start()
+
+    def prepare_t(i, carry):
+        slot = lax.rem(i, 2)
+        fetch_t(i, slot).wait()
+
+        @pl.when(i + 1 < chunks)
+        def _():
+            fetch_t(i + 1, 1 - slot).start()
+
+        by_c = jnp.swapaxes(stage_t[slot], 0, 1)
+        at = pl.multiple_of(i * GROUP, GROUP)
+        for o in range(col_count):
+            direct[o, pl.ds(at, GROUP)] = by_c[:, :, o * columns:o * columns + LANES]
+        for t in range(GROUP // 4):
+            direct_tail[i * (GROUP // 4) + t] = jnp.concatenate(
+                [
+                    by_c[4 * t + c, :, o * columns + LANES:(o + 1) * columns]
+                    for c in range(4) for o in range(col_count)
+                ],
+                axis=1,
+            )
+        return carry
+
+    lax.fori_loop(0, chunks, prepare_t, 0)
+
+    for j in range(WIN):
+        own(j).wait_recv()
+        near(1, j).start()
+        near(2, j).start()
+    shared(3).start()
+    own_flip.wait()
+    own_tail.wait()
+
+    def prepare_b(i, carry):
+        slot = lax.rem(i, 2)
+        fetch_b(i, slot).wait()
+
+        @pl.when(i + 1 < chunks)
+        def _():
+            fetch_b(i + 1, 1 - slot).start()
+
+        by_c = jnp.swapaxes(stage_b[slot].astype(jnp.float32), 0, 1).reshape(span, depth)
+        slabs[pl.ds(pl.multiple_of(i * span, LANES), span), :] = by_c.astype(jnp.bfloat16)
+        return carry
+
+    lax.fori_loop(0, chunks, prepare_b, 0)
+    out_ref[...] = jnp.zeros_like(out_ref)
+
+    def piece(k, carry):
+        @pl.when(k == 1)
+        def _():
+            for j in range(WIN):
+                near(1, j).wait_recv()
+                near(2, j).wait_recv()
+            for j in range(WIN):
+                far(j).start()
+            for p in range(1, 4):
+                tails(p).start()
+            for p in range(1, 4):
+                relay(p).wait_recv()
+                pair(p, 0).start()
+                pair(p, 1).start()
+            for h in range(2):
+                pair(1, h).wait_recv()
+
+        @pl.when(k == 2)
+        def _():
+            for h in range(2):
+                pair(2, h).wait_recv()
+
+        @pl.when(k == 3)
+        def _():
+            for j in range(WIN):
+                far(j).wait_recv()
+            for h in range(2):
+                pair(3, h).wait_recv()
+
+        kx, ky = lax.rem(k, 2), k // 2
+        origin = (qy + ky - 2 * qy * ky) * 2 + (qx + kx - 2 * qx * kx)
+
+        def chunk(i, inner):
+            @pl.when((k == 0) & (i == chunks // 2))
+            def _():
+                for p in range(1, 4):
+                    shared(p).wait_recv()
+                    relay(p).start()
+
+            lhs = slabs[pl.ds(pl.multiple_of(i * span, LANES), span), :]
+            rhs = jnp.concatenate([window[k, j, :LANES, :] for j in range(WIN)], axis=0)
+            tiled[...] = matmul_nt(lhs, rhs)
+            total = out_ref[...]
+            for c in range(0, GROUP, 2):
+                at = i * GROUP + c
+                stacked = jnp.concatenate(
+                    [
+                        jnp.concatenate(
+                            [
+                                tiled[(c + h) * rows:(c + h + 1) * rows, j * LANES:(j + 1) * LANES]
+                                for h in range(2)
+                            ],
+                            axis=1,
+                        )
+                        for j in range(WIN)
+                    ],
+                    axis=0,
+                ).astype(jnp.bfloat16)
+                both = jnp.concatenate(
+                    [
+                        jnp.concatenate([direct[origin, at], direct[origin, at + 1]], axis=1),
+                        jnp.concatenate([flipped[k, at], flipped[k, at + 1]], axis=1),
+                    ],
+                    axis=0,
+                )
+                total += matmul_nt(stacked, both)
+            out_ref[...] = total
+            return inner
+
+        lax.fori_loop(0, chunks, chunk, 0)
+        return carry
+
+    lax.fori_loop(0, col_count, piece, 0)
+
+    for k in range(1, 4):
+        tails(k).wait_recv()
+    step = WIN * extra
+
+    def place(o):
+        kx, ky = o % 2, o // 2
+        return (qy + ky - 2 * qy * ky) * 2 + (qx + kx - 2 * qx * kx)
+
+    def tail_chunk(i, carry):
+        lhs = slabs[pl.ds(pl.multiple_of(i * span, LANES), span), :]
+        rhs = jnp.concatenate(
+            [window[place(o), j, LANES:, :] for j in range(WIN) for o in range(col_count)], axis=0
+        )
+        tiled[:, :WIN * step] = matmul_nt(lhs, rhs)
+        total = out_ref[...]
+        for t in range(GROUP // 4):
+            stacked = jnp.concatenate(
+                [
+                    jnp.concatenate(
+                        [
+                            tiled[(4 * t + c) * rows:(4 * t + c + 1) * rows, j * step:(j + 1) * step]
+                            for c in range(4)
+                        ],
+                        axis=1,
+                    )
+                    for j in range(WIN)
+                ],
+                axis=0,
+            ).astype(jnp.bfloat16)
+            first = 4 * (t % 2)
+            back = jnp.concatenate(
+                [
+                    flipped_tail[place(o), i * (GROUP // 8) + t // 2, :, (first + c) * extra:(first + c + 1) * extra]
+                    for c in range(4) for o in range(col_count)
+                ],
+                axis=1,
+            )
+            both = jnp.concatenate([direct_tail[i * (GROUP // 4) + t], back], axis=0)
+            total += matmul_nt(stacked, both)
+        out_ref[...] = total
+        return carry
+
+    lax.fori_loop(0, chunks, tail_chunk, 0)
+
+    for k in range(1, 4):
+        sums(k).start()
+    for j in range(WIN):
+        own(j).wait_send()
+        near(1, j).wait_send()
+        near(2, j).wait_send()
+        far(j).wait_send()
+    for k in range(1, 4):
+        shared(k).wait_send()
+        relay(k).wait_send()
+        pair(k, 0).wait_send()
+        pair(k, 1).wait_send()
+        tails(k).wait_send()
+    for k in range(1, 4):
+        sums(k).wait()
+    out_ref[...] = (out_ref[...] + parts[0]) + (parts[1] + parts[2])
+
+
+def fused(df_blocks, amplitudes):
+    rows, columns, depth = df_blocks.shape
+    pairs, _, extent = amplitudes.shape
+    row_count, col_count = lax.axis_size("row"), lax.axis_size("col")
+    extra = columns - LANES
+    flip = amplitudes[:, :LANES, :].transpose(2, 0, 1)
+    flip_tail = amplitudes[:, LANES:, :].reshape(pairs, extra, extent // 8, 8)
+    flip_tail = flip_tail.transpose(2, 0, 3, 1).reshape(extent // 8, pairs, 8 * extra)
+    dma = pltpu.SemaphoreType.DMA
+    bf16 = jnp.bfloat16
+    total = pl.pallas_call(
+        functools.partial(fused_kernel, row_count, col_count),
+        out_shape=jax.ShapeDtypeStruct((WIN * rows, 2 * pairs), jnp.float32),
+        in_specs=[pl.BlockSpec(memory_space=pltpu.HBM)] * 4,
+        out_specs=pl.BlockSpec(memory_space=pltpu.VMEM),
+        scratch_shapes=[
+            pltpu.VMEM((columns * rows, depth), bf16),
+            pltpu.VMEM((col_count, WIN, columns, depth), bf16),
+            pltpu.VMEM((GROUP * rows, WIN * LANES), jnp.float32),
+            pltpu.VMEM((col_count, columns, pairs, LANES), bf16),
+            pltpu.VMEM((columns // 4, pairs, 4 * col_count * extra), bf16),
+            pltpu.VMEM((col_count, columns, pairs, LANES), bf16),
+            pltpu.VMEM((col_count, columns // 8, pairs, LANES), bf16),
+            pltpu.VMEM((2, rows, GROUP, depth), bf16),
+            pltpu.VMEM((2, pairs, GROUP, extent), bf16),
+            pltpu.VMEM((3, WIN * rows, 2 * pairs), jnp.float32),
+            dma((4,)), dma((4,)), dma((2, 4)), dma((2, 4)), dma((4,)), dma((4,)),
+            dma((3,)), dma((3,)), dma((3,)), dma((3,)), dma((3, 2)), dma((3, 2)),
+            dma((3,)), dma((3,)), dma((3,)), dma((3,)), dma((2,)), dma((2,)), dma((2,)),
+        ],
+        compiler_params=pltpu.CompilerParams(
+            collective_id=0, has_side_effects=True, vmem_limit_bytes=67043328
+        ),
+    )(df_blocks, amplitudes, flip, flip_tail)
+    total = total.reshape(WIN, rows, 2 * pairs).transpose(1, 0, 2)
+    return (total[:, :, :pairs], total[:, :, pairs:])
+
+
+def fits_fused(df_blocks, amplitudes):
+    rows, columns, depth = df_blocks.shape
+    pairs, _, extent = amplitudes.shape
+    row_count, col_count = lax.axis_size("row"), lax.axis_size("col")
+    extra = columns - LANES
+    return (
+        col_count == 4 and row_count % SHARES == 0 and row_count >= 4 and rows % 8 == 0 and rows >= WIN
+        and columns % GROUP == 0 and columns % SHARES == 0 and extra == 16 and WIN == 4
+        and pairs % 16 == 0 and depth % LANES == 0 and GROUP * rows % LANES == 0
+    )
+
+
 def shards(df_blocks, amplitudes):
+    if fits_fused(df_blocks, amplitudes):
+        return fused(df_blocks, amplitudes)
     rows, columns, depth = df_blocks.shape
     pairs, _, extent = amplitudes.shape
     row_count = lax.axis_size("row")

time: 386 us -> 176 us (0.46)
  the two profiles are of different devices: /device:TPU:0 before, /device:TPU:9 now
where the time goes in v1:
time: 176 us; the launch traced here: 175 us
  Pallas kernels  146 us (83%)
  local copies, waits for them, and re-layouts  29.1 us (17%)
    pallas_call x1, Pallas kernels, fused(): pl.pallas_call(functools.partial(fused_kernel, row_count, col_count), out...  146 us
    unnamed x1, local copies, waits for them, and re-layouts  11 us
    slice x1, local copies, waits for them, and re-layouts, fused(): flip = amplitudes[:, :LANES, :].transpose(2, 0, 1)  7.56 us
    transpose x1, local copies, waits for them, and re-layouts, fused(): flip_tail.transpose(2, 0, 3, 1).reshape(extent // 8, pairs, 8 * extra)  4.08 us

profile of v1, /device:TPU:9, one launch (start us, length us, event | category | flops | bytes accessed | tf_op | source)
XLA Modules:
  0.0 175.3 jit_solution(6108491524861852840)
XLA Ops:
  0.6 7.6 %slice.12 = bf16[48,128,576]{2,1,0:T(8,128)(2,1)} slice(bf16[48,144,576]{2,1,0:T(8,128)(2,1)} %amps_ref.1), slice={[0:48], [0:128], [0:576]} | slice | bytes 14155776 | tf_op jit(solution)/shard_map/slice | solution.py:373
  8.2 0.0 slice-start
  8.2 11.0 %copy.12 = bf16[48,128,576]{1,0,2:T(8,128)(2,1)} copy(bf16[48,128,576]{2,1,0:T(8,128)(2,1)} %slice.12) | data formatting | bytes 14155776
  19.2 0.0 slice-done
  19.2 2.1 %copy.8 = bf16[48,16,576]{0,2,1:T(8,128)(2,1)S(1)} copy(bf16[48,16,576]{2,1,0:T(8,128)(2,1)S(1)} %slice-done) | data formatting | bytes 1769472 | tf_op jit(solution)/shard_map/slice | solution.py:374
  21.4 4.1 %copy.9 = bf16[72,48,8,16]{0,3,2,1:T(8,128)(2,1)} copy(bf16[72,48,8,16]{1,2,0,3:T(8,128)(2,1)S(1)} %bitcast.8) | data formatting | bytes 1769472 | tf_op jit(solution)/shard_map/transpose | solution.py:375
  25.4 2.6 %copy.10.flip_tail_ref = bf16[72,48,128]{2,1,0:T(8,128)(2,1)} copy(bf16[72,48,128]{0,2,1:T(8,128)(2,1)} %bitcast.9) | data formatting | bytes 1769472 | tf_op jit(solution)/shard_map/reshape | solution.py:375
  28.0 145.6 %shard_map.41 = f32[288,96]{1,0:T(8,128)} custom-call(bf16[72,144,1024]{2,1,0:T(8,128)(2,1)} %df_ref.1, bf16[48,144,576]{2,1,0:T(8,128)(2,1)} %amps_ref.1, bf16[576,48,128]{2,1,0:T(8,128)(2,1)} %bitcast.7, bf16[72,48,128]{2,1,0:T(8,128)(2,1)} %copy.10.flip_tail_ref), custom_call_target="tpu_custom_call" | custom-call | tf_op jit(solution)/shard_map/pallas_call | solution.py:378
  173.6 1.0 copy.11
  174.6 0.7 fusion
Async XLA Ops:
  8.2 11.0 %slice-start = ((bf16[48,144,576]{2,1,0:T(8,128)(2,1)}), bf16[48,16,576]{2,1,0:T(8,128)(2,1)S(1)}, s32[]{:S(2)}) async-start(bf16[48,144,576]{2,1,0:T(8,128)(2,1)} %amps_ref.1), calls=%async_computation | async-start | bytes 1966080 | tf_op jit(solution)/shard_map/slice | solution.py:374

commit v2 on v1

--- a/solution.py
+++ b/solution.py
@@ -94,18 +94,20 @@
 
 
 def fused_kernel(
-    row_count, col_count, df_ref, amps_ref, flip_ref, flip_tail_ref, out_ref,
-    slabs, window, tiled, direct, direct_tail, flipped, flipped_tail, stage_b, stage_t, parts,
+    row_count, col_count, df_ref, amps_ref, out_ref,
+    slabs, window, tiled, direct, direct_tail, flipped, flipped_tail, flip_out, tail_out, stage_b, stage_t, stage_f, parts,
     own_s, own_r, near_s, near_r, far_s, far_r, share_s, share_r, relay_s, relay_r, pair_s, pair_r,
-    tail_s, tail_r, sum_s, sum_r, local, stage_b_sem, stage_t_sem,
+    sum_s, sum_r, stage_b_sem, stage_t_sem, stage_f_sem,
 ):
     rows, columns, depth = df_ref.shape
     pairs = amps_ref.shape[0]
     extra = columns - LANES
     chunks = columns // GROUP
     span = GROUP * rows
-    share = columns // SHARES
-    octets = flip_tail_ref.shape[0] // col_count
+    extent = amps_ref.shape[2]
+    octets = columns // 8
+    share = pairs // SHARES
+    padded = flip_out.shape[1]
     r, q = lax.axis_index("row"), lax.axis_index("col")
     below, above = lax.rem(r + row_count - 1, row_count), lax.rem(r + 1, row_count)
     slot_r = lax.rem(r, SHARES)
@@ -134,25 +136,45 @@
         k = 1 if j < 2 else 2
         return remote(window.at[k, j], window.at[3, j], far_s.at[j], far_r.at[j], r, peers[3 - k])
 
-    def share_at(s):
-        return pl.ds(s * share, share)
+    def at_share(s):
+        return pl.ds(pl.multiple_of(s * padded, padded), padded)
+
+    def both_parts(k, make):
+        return (make(flipped.at[k], 0), make(flipped_tail.at[k], 1))
 
     def shared(k):
-        src = flip_ref.at[pl.ds(peers[k] * columns + slot_r * share, share)]
-        return remote(src, flipped.at[k, share_at(slot_r)], share_s.at[k - 1], share_r.at[k - 1], r, peers[k])
+        def make(ref, t):
+            size = octets if t else columns
+            src = (tail_out if t else flip_out).at[pl.ds(peers[k] * size, size)]
+            dst = ref.at[:, at_share(slot_r), :]
+            return remote(src, dst, share_s.at[k - 1, t], share_r.at[k - 1, t], r, peers[k])
+        return both_parts(k, make)
 
     def relay(k):
-        ref = flipped.at[k, share_at(slot_r)]
-        return remote(ref, ref, relay_s.at[k - 1], relay_r.at[k - 1], twin, q)
+        def make(ref, t):
+            ref = ref.at[:, at_share(slot_r), :]
+            return remote(ref, ref, relay_s.at[k, t], relay_r.at[k, t], twin, q)
+        return both_parts(k, make)
 
     def pair(k, h):
         s = slot_r if h == 0 else lax.rem(twin, SHARES)
-        ref = flipped.at[k, share_at(s)]
-        return remote(ref, ref, pair_s.at[k - 1, h], pair_r.at[k - 1, h], mate, q)
-
-    def tails(k):
-        src = flip_tail_ref.at[pl.ds(peers[k] * octets, octets)]
-        return remote(src, flipped_tail.at[k], tail_s.at[k - 1], tail_r.at[k - 1], r, peers[k])
+
+        def make(ref, t):
+            ref = ref.at[:, at_share(s), :]
+            return remote(ref, ref, pair_s.at[k, h, t], pair_r.at[k, h, t], mate, q)
+        return both_parts(k, make)
+
+    def start(copies):
+        for copy in copies:
+            copy.start()
+
+    def wait_recv(copies):
+        for copy in copies:
+            copy.wait_recv()
+
+    def wait_send(copies):
+        for copy in copies:
+            copy.wait_send()
 
     def sums(k):
         return remote(out_ref, parts.at[k - 1], sum_s.at[k - 1], sum_r.at[k - 1], r, peers[k])
@@ -167,10 +189,8 @@
 
     fetch_t(0, 0).start()
     fetch_b(0, 0).start()
-    own_flip = pltpu.make_async_copy(flip_ref.at[pl.ds(q * columns, columns)], flipped.at[0], local.at[0])
-    own_tail = pltpu.make_async_copy(flip_tail_ref.at[pl.ds(q * octets, octets)], flipped_tail.at[0], local.at[1])
-    own_flip.start()
-    own_tail.start()
+    fetch_f = pltpu.make_async_copy(amps_ref.at[pl.ds(slot_r * share, share)], stage_f, stage_f_sem.at[0])
+    fetch_f.start()
 
     barrier = pltpu.get_barrier_semaphore()
     for dr, dq in ((below, q), (above, q), (twin, q), (r, x_q), (r, y_q), (r, d_q)):
@@ -179,8 +199,33 @@
 
     for j in range(WIN):
         own(j).start()
-    shared(1).start()
-    shared(2).start()
+    fetch_f.wait()
+    blank = jnp.zeros((extent, columns), jnp.bfloat16)
+    for at in range(0, extent, LANES):
+        size = min(LANES, extent - at)
+        turned = jnp.stack(
+            [stage_f[p, :, at:at + size].T for p in range(share)] + [blank[:size]] * (padded - share), axis=0
+        )
+        by_d = jnp.swapaxes(turned, 0, 1)
+        flip_out[at:at + size] = by_d[:, :, :LANES]
+        for o in range(size // 8):
+            tail_out[at // 8 + o] = jnp.concatenate([by_d[8 * o + c, :, LANES:] for c in range(8)], axis=1)
+    flipped[0, :, at_share(slot_r), :] = flip_out[pl.ds(q * columns, columns)]
+    flipped_tail[0, :, at_share(slot_r), :] = tail_out[pl.ds(q * octets, octets)]
+
+    def forward_window():
+        for j in range(WIN):
+            own(j).wait_recv()
+            near(1, j).start()
+            near(2, j).start()
+
+    start(relay(0))
+    start(shared(1))
+    start(shared(2))
+
+    @pl.when(odd == 0)
+    def _():
+        forward_window()
 
     def prepare_t(i, carry):
         slot = lax.rem(i, 2)
@@ -206,13 +251,11 @@
 
     lax.fori_loop(0, chunks, prepare_t, 0)
 
-    for j in range(WIN):
-        own(j).wait_recv()
-        near(1, j).start()
-        near(2, j).start()
-    shared(3).start()
-    own_flip.wait()
-    own_tail.wait()
+    @pl.when(odd == 1)
+    def _():
+        forward_window()
+
+    start(shared(3))
 
     def prepare_b(i, carry):
         slot = lax.rem(i, 2)
@@ -227,6 +270,14 @@
         return carry
 
     lax.fori_loop(0, chunks, prepare_b, 0)
+    wait_recv(relay(0))
+    for h in range(2):
+        start(pair(0, h))
+    for p in (1, 2):
+        wait_recv(shared(p))
+        start(relay(p))
+    for h in range(2):
+        wait_recv(pair(0, h))
     out_ref[...] = jnp.zeros_like(out_ref)
 
     def piece(k, carry):
@@ -237,41 +288,47 @@
                 near(2, j).wait_recv()
             for j in range(WIN):
                 far(j).start()
-            for p in range(1, 4):
-                tails(p).start()
-            for p in range(1, 4):
-                relay(p).wait_recv()
-                pair(p, 0).start()
-                pair(p, 1).start()
             for h in range(2):
-                pair(1, h).wait_recv()
+                wait_recv(pair(1, h))
 
         @pl.when(k == 2)
         def _():
             for h in range(2):
-                pair(2, h).wait_recv()
+                wait_recv(pair(2, h))
 
         @pl.when(k == 3)
         def _():
             for j in range(WIN):
                 far(j).wait_recv()
             for h in range(2):
-                pair(3, h).wait_recv()
+                wait_recv(pair(3, h))
 
         kx, ky = lax.rem(k, 2), k // 2
         origin = (qy + ky - 2 * qy * ky) * 2 + (qx + kx - 2 * qx * kx)
 
         def chunk(i, inner):
-            @pl.when((k == 0) & (i == chunks // 2))
+            @pl.when((k == 0) & (i == chunks - 2))
             def _():
-                for p in range(1, 4):
-                    shared(p).wait_recv()
-                    relay(p).start()
+                for p in (1, 2):
+                    wait_recv(relay(p))
+                    for h in range(2):
+                        start(pair(p, h))
+
+            @pl.when((k == 1) & (i == chunks - 3))
+            def _():
+                wait_recv(shared(3))
+                start(relay(3))
+
+            @pl.when((k == 2) & (i == chunks - 2))
+            def _():
+                wait_recv(relay(3))
+                for h in range(2):
+                    start(pair(3, h))
 
             lhs = slabs[pl.ds(pl.multiple_of(i * span, LANES), span), :]
             rhs = jnp.concatenate([window[k, j, :LANES, :] for j in range(WIN)], axis=0)
             tiled[...] = matmul_nt(lhs, rhs)
-            total = out_ref[...]
+            total = None
             for c in range(0, GROUP, 2):
                 at = i * GROUP + c
                 stacked = jnp.concatenate(
@@ -294,8 +351,9 @@
                     ],
                     axis=0,
                 )
-                total += matmul_nt(stacked, both)
-            out_ref[...] = total
+                term = matmul_nt(stacked, both)
+                total = term if total is None else total + term
+            out_ref[...] += total
             return inner
 
         lax.fori_loop(0, chunks, chunk, 0)
@@ -303,8 +361,6 @@
 
     lax.fori_loop(0, col_count, piece, 0)
 
-    for k in range(1, 4):
-        tails(k).wait_recv()
     step = WIN * extra
 
     def place(o):
@@ -317,7 +373,7 @@
             [window[place(o), j, LANES:, :] for j in range(WIN) for o in range(col_count)], axis=0
         )
         tiled[:, :WIN * step] = matmul_nt(lhs, rhs)
-        total = out_ref[...]
+        total = None
         for t in range(GROUP // 4):
             stacked = jnp.concatenate(
                 [
@@ -341,8 +397,9 @@
                 axis=1,
             )
             both = jnp.concatenate([direct_tail[i * (GROUP // 4) + t], back], axis=0)
-            total += matmul_nt(stacked, both)
-        out_ref[...] = total
+            term = matmul_nt(stacked, both)
+            total = term if total is None else total + term
+        out_ref[...] += total
         return carry
 
     lax.fori_loop(0, chunks, tail_chunk, 0)
@@ -354,12 +411,12 @@
         near(1, j).wait_send()
         near(2, j).wait_send()
         far(j).wait_send()
-    for k in range(1, 4):
-        shared(k).wait_send()
-        relay(k).wait_send()
-        pair(k, 0).wait_send()
-        pair(k, 1).wait_send()
-        tails(k).wait_send()
+    for k in range(4):
+        wait_send(relay(k))
+        wait_send(pair(k, 0))
+        wait_send(pair(k, 1))
+        if k:
+            wait_send(shared(k))
     for k in range(1, 4):
         sums(k).wait()
     out_ref[...] = (out_ref[...] + parts[0]) + (parts[1] + parts[2])
@@ -370,15 +427,14 @@
     pairs, _, extent = amplitudes.shape
     row_count, col_count = lax.axis_size("row"), lax.axis_size("col")
     extra = columns - LANES
-    flip = amplitudes[:, :LANES, :].transpose(2, 0, 1)
-    flip_tail = amplitudes[:, LANES:, :].reshape(pairs, extra, extent // 8, 8)
-    flip_tail = flip_tail.transpose(2, 0, 3, 1).reshape(extent // 8, pairs, 8 * extra)
+    padded = -(-(pairs // SHARES) // 16) * 16
+    width = pairs + SHARES * padded
     dma = pltpu.SemaphoreType.DMA
     bf16 = jnp.bfloat16
     total = pl.pallas_call(
         functools.partial(fused_kernel, row_count, col_count),
-        out_shape=jax.ShapeDtypeStruct((WIN * rows, 2 * pairs), jnp.float32),
-        in_specs=[pl.BlockSpec(memory_space=pltpu.HBM)] * 4,
+        out_shape=jax.ShapeDtypeStruct((WIN * rows, width), jnp.float32),
+        in_specs=[pl.BlockSpec(memory_space=pltpu.HBM)] * 2,
         out_specs=pl.BlockSpec(memory_space=pltpu.VMEM),
         scratch_shapes=[
             pltpu.VMEM((columns * rows, depth), bf16),
@@ -386,21 +442,25 @@
             pltpu.VMEM((GROUP * rows, WIN * LANES), jnp.float32),
             pltpu.VMEM((col_count, columns, pairs, LANES), bf16),
             pltpu.VMEM((columns // 4, pairs, 4 * col_count * extra), bf16),
-            pltpu.VMEM((col_count, columns, pairs, LANES), bf16),
-            pltpu.VMEM((col_count, columns // 8, pairs, LANES), bf16),
+            pltpu.VMEM((col_count, columns, SHARES * padded, LANES), bf16),
+            pltpu.VMEM((col_count, columns // 8, SHARES * padded, LANES), bf16),
+            pltpu.VMEM((extent, padded, LANES), bf16),
+            pltpu.VMEM((extent // 8, padded, LANES), bf16),
             pltpu.VMEM((2, rows, GROUP, depth), bf16),
             pltpu.VMEM((2, pairs, GROUP, extent), bf16),
-            pltpu.VMEM((3, WIN * rows, 2 * pairs), jnp.float32),
+            pltpu.VMEM((pairs // SHARES, columns, extent), bf16),
+            pltpu.VMEM((3, WIN * rows, width), jnp.float32),
             dma((4,)), dma((4,)), dma((2, 4)), dma((2, 4)), dma((4,)), dma((4,)),
-            dma((3,)), dma((3,)), dma((3,)), dma((3,)), dma((3, 2)), dma((3, 2)),
-            dma((3,)), dma((3,)), dma((3,)), dma((3,)), dma((2,)), dma((2,)), dma((2,)),
+            dma((3, 2)), dma((3, 2)), dma((4, 2)), dma((4, 2)), dma((4, 2, 2)), dma((4, 2, 2)),
+            dma((3,)), dma((3,)), dma((2,)), dma((2,)), dma((1,)),
         ],
         compiler_params=pltpu.CompilerParams(
             collective_id=0, has_side_effects=True, vmem_limit_bytes=67043328
         ),
-    )(df_blocks, amplitudes, flip, flip_tail)
-    total = total.reshape(WIN, rows, 2 * pairs).transpose(1, 0, 2)
-    return (total[:, :, :pairs], total[:, :, pairs:])
+    )(df_blocks, amplitudes)
+    total = total.reshape(WIN, rows, width).transpose(1, 0, 2)
+    back = total[:, :, pairs:].reshape(rows, WIN, SHARES, padded)[..., :pairs // SHARES]
+    return (total[:, :, :pairs], back.reshape(rows, WIN, pairs))
 
 
 def fits_fused(df_blocks, amplitudes):
@@ -410,7 +470,7 @@
     extra = columns - LANES
     return (
         col_count == 4 and row_count % SHARES == 0 and row_count >= 4 and rows % 8 == 0 and rows >= WIN
-        and columns % GROUP == 0 and columns % SHARES == 0 and extra == 16 and WIN == 4
+        and columns % GROUP == 0 and pairs % SHARES == 0 and extent % 64 == 0 and extra == 16 and WIN == 4
         and pairs % 16 == 0 and depth % LANES == 0 and GROUP * rows % LANES == 0
     )
 

time: 176 us -> 143 us (0.81)
  the two profiles are of different devices: /device:TPU:9 before, /device:TPU:0 now
where the time goes in v2:
time: 143 us; the launch traced here: 142 us
  Pallas kernels  139 us (97%)
  local copies, waits for them, and re-layouts  2.4 us (2%)
    pallas_call x1, Pallas kernels, fused(): pl.pallas_call(functools.partial(fused_kernel, row_count, col_count), out...  139 us

profile of v2, /device:TPU:0, one launch (start us, length us, event | category | flops | bytes accessed | tf_op | source)
XLA Modules:
  0.0 142.3 jit_solution(17278566929593366485)
XLA Ops:
  0.6 139.3 %shard_map.41 = f32[288,112]{1,0:T(8,128)} custom-call(bf16[72,144,1024]{2,1,0:T(8,128)(2,1)} %df_ref.1, bf16[48,144,576]{2,1,0:T(8,128)(2,1)} %amps_ref.1), custom_call_target="tpu_custom_call" | custom-call | tf_op jit(solution)/shard_map/pallas_call | solution.py:434
  139.9 1.0 copy.5
  140.9 0.7 slice.12
  141.6 0.1 copy.8
  141.7 0.6 copy.7
  (1 shorter events, 0.0 us)
